TPU v7x, 128 devices: a whole 4x4x4 slice. The times are simulated.
128 devices in a mesh: row: 8 (over x, core), col: 4 (over z), layer: 4 (over y).
Axes of the slice: x: 4, y: 4, z: 4, core: 2. Of those that a mesh axis runs over, the one named last changes fastest.
Arguments:
- a_blocks: float32 [8, 128, 128, 128], P('row', ('col', 'layer')), may hold values from -0.5 to 0.5
- b_blocks: float32 [128, 4, 128, 128], P(('row', 'layer'), 'col'), may hold values from -2.5 to 2.5
- pair_plan: int32 [8, 4, 4, 8, 4, 3, 16], P('row', 'col', 'layer'), may hold values from 0 to 127, as said below
- pair_counts: int32 [8, 4, 4, 8, 4], P('row', 'col', 'layer'), may hold values from 0 to 16, as said below
Outputs:
- next_blocks: float32 [8, 4, 128, 128, 128], P('row', 'col', 'layer')
Inputs may be any that keep to these rules, and one draw needn't show every extreme that they name: `pair_plan`: field 0 names a block of a_blocks whose index divided by 8 (rounded down) is congruent to m modulo 4; field 1 lies in 0 to 3 and field 2 in 0 to 31; entries past the count obey the same ranges. `pair_counts`: some entry equals 16 in every draw.
All inputs are finite; a program needn't handle non-finite values.
Results may differ from a plain program's by a relative error of at most 0.0003.
Values sent between devices are 32-bit elements; how exact they have to be, the bound alone decides.
A program may use at most 128 MiB of HBM per device.

v0:
```python
import jax
import jax.numpy as jnp
from jax import lax
from jax.sharding import PartitionSpec as P

BS = 128
ACAP = 8
BCAP = 4
CL = 32


def side_by_side(arrays, axis, split_dim, concat_dim, along):
    columns = [a.reshape(*a.shape[:along], -1) for a in arrays]
    both = jnp.concatenate(columns, axis=along)
    out, at, finished = (
        lax.all_to_all(both, axis, split_axis=split_dim, concat_axis=concat_dim, tiled=True),
        0,
        [],
    )
    for a, column in zip(arrays, columns):
        slab = out[..., at : at + column.shape[along]]
        finished.append(slab.reshape(*slab.shape[:along], *a.shape[along:]))
        at += column.shape[along]
    return tuple(finished)


def copy_for_each(value, axis):
    copies = jnp.broadcast_to(value, (lax.axis_size(axis), *value.shape))
    return lax.all_to_all(copies, axis, split_axis=0, concat_axis=0, tiled=True)


def joined_along(blocks, dim):
    lengths = list(blocks.shape[1:])
    lengths[dim] *= blocks.shape[0]
    return jnp.moveaxis(blocks, 0, dim).reshape(lengths)


def gather_directly(value, axis, dim):
    blocks = copy_for_each(value, axis)
    return joined_along(blocks, dim)


def add_pairs(totals, left_blocks, right_blocks, left_ids, right_ids, target, live):
    lhs = jnp.take(left_blocks, left_ids, axis=0)
    rhs = jnp.take(right_blocks, right_ids, axis=0)
    products = jnp.einsum("pij,pjk->pik", lhs, rhs, precision=lax.Precision.HIGHEST)
    products = jnp.where(live[:, None, None], products, jnp.zeros_like(products))
    return totals.at[target].add(products)


def accumulate(totals, left_blocks, right_blocks, entries, numbers, offsets):
    extent = entries.shape[2]
    live = (jnp.arange(extent, dtype=jnp.int32)[None, :] < numbers[:, None]).reshape(-1)
    target = (entries[:, 2] + offsets[:, None]).reshape(-1)
    return add_pairs(
        totals,
        left_blocks,
        right_blocks,
        entries[:, 0].reshape(-1),
        entries[:, 1].reshape(-1),
        target,
        live,
    )


def sweep(totals, piece, groups, group_counts, offsets, left_blocks):
    shards = piece.shape[0] // BCAP

    def per_shard(index, running):
        blocks = lax.dynamic_slice_in_dim(piece, index * BCAP, BCAP, 0)[:, 0]
        entries = lax.dynamic_index_in_dim(groups, index, 0, keepdims=False)
        numbers = lax.dynamic_index_in_dim(group_counts, index, 0, keepdims=False)
        return accumulate(running, left_blocks, blocks, entries, numbers, offsets)

    return lax.fori_loop(0, shards, per_shard, totals)


def per_device(a_blocks, b_blocks, pair_plan, pair_counts):
    layer_count = lax.axis_size("layer")
    plan = pair_plan[0, 0, 0]
    counts = pair_counts[0, 0, 0]
    plan_here, counts_here = side_by_side((plan, counts), "layer", 1, 1, 2)
    left_ids = plan_here[:, :, 0]
    local_ids = left_ids // (layer_count * ACAP) * ACAP + left_ids % ACAP
    plan_here = jnp.stack([local_ids, plan_here[:, :, 1], plan_here[:, :, 2]], axis=2)
    left_blocks = lax.all_gather(a_blocks, "col", axis=1, tiled=True)[0]
    offsets = jnp.arange(layer_count, dtype=jnp.int32) * CL
    initial = jnp.zeros((layer_count * CL, BS, BS), jnp.float32)
    partial_value = sweep(
        initial, gather_directly(b_blocks, "row", 0), plan_here, counts_here, offsets, left_blocks
    )
    result = lax.psum_scatter(partial_value, "layer", scatter_dimension=0, tiled=True)
    return result[None, None]


def solution(mesh):
    in_specs = (
        P("row", ("col", "layer"), None, None),
        P(("row", "layer"), "col", None, None),
        P("row", "col", "layer", None, None, None, None),
        P("row", "col", "layer", None, None),
    )
    out_specs = P("row", "col", "layer", None, None)
    return jax.shard_map(
        per_device, mesh=mesh, in_specs=in_specs, out_specs=out_specs, check_vma=False
    )
```

profile of v0, /device:TPU:0, one launch (start us, length us, event | category | flops | bytes accessed | tf_op | source)
XLA Modules:
  0.0 390.6 jit_solution(7997675835676705044)
XLA Ops:
  6.5 0.7 all-gather.2.cloned.1.call-update
  7.3 0.8 copy.15
  8.0 0.8 copy.14
  8.8 0.1 reshape_squeeze.6
  9.0 0.1 reshape.181
  9.1 9.7 %all_to_all.10 = s32[4,1,392]{2,1,0:T(1,128)S(1)} all-to-all(s32[4,1,392]{2,1,0:T(1,128)S(1)} %reshape.181), channel_id=1, replica_groups=mesh['row'=8,'col'=4,'layer'=4] {'layer'}, dimensions={0} | all-to-all | bytes 12544 | tf_op jit(solution)/shard_map/all_to_all | solution.py:16
  18.8 2.5 broadcast_in_dim.74
  21.3 4.3 %all-to-all-start.1 = ((f32[8,4,1,128,128]{4,3,1,2,0:T(8,128)}), f32[8,4,1,128,128]{4,3,1,2,0:T(8,128)S(1)}, u32[]{:S(2)}, u32[]{:S(2)}) async-start(f32[8,4,1,128,128]{4,3,1,2,0:T(8,128)} %broadcast_in_dim.74), calls=%async_computation.1 | async-start | bytes 4194304 | tf_op jit(solution)/shard_map/all_to_all | solution.py:29
  25.7 0.5 broadcast.173
  26.2 0.6 reduce
  26.9 0.1 copy.20
  27.1 0.1 reshape.145
  27.2 0.1 fusion.17
  27.4 25.4 %all-to-all-done.1 = f32[8,4,1,128,128]{4,3,1,2,0:T(8,128)S(1)} async-done(((f32[8,4,1,128,128]{4,3,1,2,0:T(8,128)}), f32[8,4,1,128,128]{4,3,1,2,0:T(8,128)S(1)}, u32[]{:S(2)}, u32[]{:S(2)}) %all-to-all-start.1) | async-done | bytes 2097184 | tf_op jit(solution)/shard_map/all_to_all | solution.py:29
  52.8 1.3 copy-done.1
  54.1 4.3 %broadcast_in_dim.73 = f32[128,128,128]{2,1,0:T(8,128)} broadcast(f32[]{:T(128)} %constant.123.clone.1), dimensions={} | broadcast | bytes 8388612 | tf_op jit(solution)/shard_map/broadcast_in_dim | solution.py:88
  58.4 246.4 %while.14 = (s32[]{:T(128)}, f32[128,128,128]{2,1,0:T(8,128)}, s32[8,4,3,16]{3,1,2,0:T(4,128)S(1)}, s32[8,4]{1,0:T(8,128)S(1)}, f32[32,128,128]{2,1,0:T(8,128)S(...) while((s32[]{:T(128)}, f32[128,128,128]{2,1,0:T(8,128)}, ...), condition=%wide.region_2.3_spmd.clone, body=%wide.region_0.2_spmd.clone.sunk | while | flops 1614810624 | bytes 42486264 | solution.py:75
  58.5 0.1 lt.176
  59.2 1.0 dynamic-slice_bitcast_fusion.5
  60.2 2.8 gather_fusion
  63.0 2.7 gather_fusion.1
  65.7 10.1 %broadcast_select_fusion.2 = f32[64,128,128]{2,1,0:T(8,128)} fusion(f32[64,128,128]{2,1,0:T(8,128)} %gather_fusion, pred[64]{0:T(512)(128)(4,1)S(1)} %get-tuple-element.235, f32[64,128,128]{2,1,0:T(8,128)} %gather_fusion.1, pred[64]{0:T(512)(128)(4,1)S(1)} %get-tuple-element.237, pred[64]{0:T(512)(128)(4,1)S(1)} %lt.176), kind=kOutput, calls=%fused_computation.7.clone.1 | convolution fusion | flops 1613758464 | bytes 12583104 | tf_op jit(solution)/shard_map/while/body/eval_jaxpr/pij,pjk->pik/dot_general | solution.py:46
  75.8 13.3 %scatter_fusion = f32[128,128,128]{2,1,0:T(8,128)} fusion(f32[128,128,128]{2,1,0:T(8,128)} %get-tuple-element.249, s32[64]{0:T(128)S(1)} %get-tuple-element.233, f32[64,128,128]{2,1,0:T(8,128)} %broadcast_select_fusion.2), kind=kCustom, calls=%fused_computation.2.clone.clone.1 | custom fusion | flops 1048576 | bytes 12583168 | tf_op jit(solution)/shard_map/while/body/eval_jaxpr/scatter-add | solution.py:48
  89.2 0.1 lt.176
  89.9 1.0 dynamic-slice_bitcast_fusion.5
  90.9 2.8 gather_fusion
  93.7 2.7 gather_fusion.1
  96.4 10.1 %broadcast_select_fusion.2 = f32[64,128,128]{2,1,0:T(8,128)} fusion(f32[64,128,128]{2,1,0:T(8,128)} %gather_fusion, pred[64]{0:T(512)(128)(4,1)S(1)} %get-tuple-element.235, f32[64,128,128]{2,1,0:T(8,128)} %gather_fusion.1, pred[64]{0:T(512)(128)(4,1)S(1)} %get-tuple-element.237, pred[64]{0:T(512)(128)(4,1)S(1)} %lt.176), kind=kOutput, calls=%fused_computation.7.clone.1 | convolution fusion | flops 1613758464 | bytes 12583104 | tf_op jit(solution)/shard_map/while/body/eval_jaxpr/pij,pjk->pik/dot_general | solution.py:46
  106.5 13.4 %scatter_fusion = f32[128,128,128]{2,1,0:T(8,128)} fusion(f32[128,128,128]{2,1,0:T(8,128)} %get-tuple-element.249, s32[64]{0:T(128)S(1)} %get-tuple-element.233, f32[64,128,128]{2,1,0:T(8,128)} %broadcast_select_fusion.2), kind=kCustom, calls=%fused_computation.2.clone.clone.1 | custom fusion | flops 1048576 | bytes 12583168 | tf_op jit(solution)/shard_map/while/body/eval_jaxpr/scatter-add | solution.py:48
  120.0 0.1 lt.176
  120.7 1.0 dynamic-slice_bitcast_fusion.5
  121.7 2.8 gather_fusion
  124.5 2.7 gather_fusion.1
  127.2 10.1 %broadcast_select_fusion.2 = f32[64,128,128]{2,1,0:T(8,128)} fusion(f32[64,128,128]{2,1,0:T(8,128)} %gather_fusion, pred[64]{0:T(512)(128)(4,1)S(1)} %get-tuple-element.235, f32[64,128,128]{2,1,0:T(8,128)} %gather_fusion.1, pred[64]{0:T(512)(128)(4,1)S(1)} %get-tuple-element.237, pred[64]{0:T(512)(128)(4,1)S(1)} %lt.176), kind=kOutput, calls=%fused_computation.7.clone.1 | convolution fusion | flops 1613758464 | bytes 12583104 | tf_op jit(solution)/shard_map/while/body/eval_jaxpr/pij,pjk->pik/dot_general | solution.py:46
  137.3 13.4 %scatter_fusion = f32[128,128,128]{2,1,0:T(8,128)} fusion(f32[128,128,128]{2,1,0:T(8,128)} %get-tuple-element.249, s32[64]{0:T(128)S(1)} %get-tuple-element.233, f32[64,128,128]{2,1,0:T(8,128)} %broadcast_select_fusion.2), kind=kCustom, calls=%fused_computation.2.clone.clone.1 | custom fusion | flops 1048576 | bytes 12583168 | tf_op jit(solution)/shard_map/while/body/eval_jaxpr/scatter-add | solution.py:48
  150.8 0.1 lt.176
  151.5 1.0 dynamic-slice_bitcast_fusion.5
  152.5 2.8 gather_fusion
  155.2 2.7 gather_fusion.1
  158.0 10.1 %broadcast_select_fusion.2 = f32[64,128,128]{2,1,0:T(8,128)} fusion(f32[64,128,128]{2,1,0:T(8,128)} %gather_fusion, pred[64]{0:T(512)(128)(4,1)S(1)} %get-tuple-element.235, f32[64,128,128]{2,1,0:T(8,128)} %gather_fusion.1, pred[64]{0:T(512)(128)(4,1)S(1)} %get-tuple-element.237, pred[64]{0:T(512)(128)(4,1)S(1)} %lt.176), kind=kOutput, calls=%fused_computation.7.clone.1 | convolution fusion | flops 1613758464 | bytes 12583104 | tf_op jit(solution)/shard_map/while/body/eval_jaxpr/pij,pjk->pik/dot_general | solution.py:46
  168.1 13.5 %scatter_fusion = f32[128,128,128]{2,1,0:T(8,128)} fusion(f32[128,128,128]{2,1,0:T(8,128)} %get-tuple-element.249, s32[64]{0:T(128)S(1)} %get-tuple-element.233, f32[64,128,128]{2,1,0:T(8,128)} %broadcast_select_fusion.2), kind=kCustom, calls=%fused_computation.2.clone.clone.1 | custom fusion | flops 1048576 | bytes 12583168 | tf_op jit(solution)/shard_map/while/body/eval_jaxpr/scatter-add | solution.py:48
  181.6 0.1 lt.176
  182.4 1.0 dynamic-slice_bitcast_fusion.5
  183.3 2.8 gather_fusion
  186.1 2.7 gather_fusion.1
  188.8 10.1 %broadcast_select_fusion.2 = f32[64,128,128]{2,1,0:T(8,128)} fusion(f32[64,128,128]{2,1,0:T(8,128)} %gather_fusion, pred[64]{0:T(512)(128)(4,1)S(1)} %get-tuple-element.235, f32[64,128,128]{2,1,0:T(8,128)} %gather_fusion.1, pred[64]{0:T(512)(128)(4,1)S(1)} %get-tuple-element.237, pred[64]{0:T(512)(128)(4,1)S(1)} %lt.176), kind=kOutput, calls=%fused_computation.7.clone.1 | convolution fusion | flops 1613758464 | bytes 12583104 | tf_op jit(solution)/shard_map/while/body/eval_jaxpr/pij,pjk->pik/dot_general | solution.py:46
  198.9 13.5 %scatter_fusion = f32[128,128,128]{2,1,0:T(8,128)} fusion(f32[128,128,128]{2,1,0:T(8,128)} %get-tuple-element.249, s32[64]{0:T(128)S(1)} %get-tuple-element.233, f32[64,128,128]{2,1,0:T(8,128)} %broadcast_select_fusion.2), kind=kCustom, calls=%fused_computation.2.clone.clone.1 | custom fusion | flops 1048576 | bytes 12583168 | tf_op jit(solution)/shard_map/while/body/eval_jaxpr/scatter-add | solution.py:48
  212.4 0.1 lt.176
  213.2 1.0 dynamic-slice_bitcast_fusion.5
  214.2 2.8 gather_fusion
  216.9 2.7 gather_fusion.1
  219.7 10.1 %broadcast_select_fusion.2 = f32[64,128,128]{2,1,0:T(8,128)} fusion(f32[64,128,128]{2,1,0:T(8,128)} %gather_fusion, pred[64]{0:T(512)(128)(4,1)S(1)} %get-tuple-element.235, f32[64,128,128]{2,1,0:T(8,128)} %gather_fusion.1, pred[64]{0:T(512)(128)(4,1)S(1)} %get-tuple-element.237, pred[64]{0:T(512)(128)(4,1)S(1)} %lt.176), kind=kOutput, calls=%fused_computation.7.clone.1 | convolution fusion | flops 1613758464 | bytes 12583104 | tf_op jit(solution)/shard_map/while/body/eval_jaxpr/pij,pjk->pik/dot_general | solution.py:46
  229.7 13.4 %scatter_fusion = f32[128,128,128]{2,1,0:T(8,128)} fusion(f32[128,128,128]{2,1,0:T(8,128)} %get-tuple-element.249, s32[64]{0:T(128)S(1)} %get-tuple-element.233, f32[64,128,128]{2,1,0:T(8,128)} %broadcast_select_fusion.2), kind=kCustom, calls=%fused_computation.2.clone.clone.1 | custom fusion | flops 1048576 | bytes 12583168 | tf_op jit(solution)/shard_map/while/body/eval_jaxpr/scatter-add | solution.py:48
  244.0 1.0 dynamic-slice_bitcast_fusion.5
  245.0 2.8 gather_fusion
  247.7 2.7 gather_fusion.1
  250.5 10.1 %broadcast_select_fusion.2 = f32[64,128,128]{2,1,0:T(8,128)} fusion(f32[64,128,128]{2,1,0:T(8,128)} %gather_fusion, pred[64]{0:T(512)(128)(4,1)S(1)} %get-tuple-element.235, f32[64,128,128]{2,1,0:T(8,128)} %gather_fusion.1, pred[64]{0:T(512)(128)(4,1)S(1)} %get-tuple-element.237, pred[64]{0:T(512)(128)(4,1)S(1)} %lt.176), kind=kOutput, calls=%fused_computation.7.clone.1 | convolution fusion | flops 1613758464 | bytes 12583104 | tf_op jit(solution)/shard_map/while/body/eval_jaxpr/pij,pjk->pik/dot_general | solution.py:46
  260.5 13.4 %scatter_fusion = f32[128,128,128]{2,1,0:T(8,128)} fusion(f32[128,128,128]{2,1,0:T(8,128)} %get-tuple-element.249, s32[64]{0:T(128)S(1)} %get-tuple-element.233, f32[64,128,128]{2,1,0:T(8,128)} %broadcast_select_fusion.2), kind=kCustom, calls=%fused_computation.2.clone.clone.1 | custom fusion | flops 1048576 | bytes 12583168 | tf_op jit(solution)/shard_map/while/body/eval_jaxpr/scatter-add | solution.py:48
  274.7 1.0 dynamic-slice_bitcast_fusion.5
  275.7 2.8 gather_fusion
  278.5 2.7 gather_fusion.1
  281.2 10.1 %broadcast_select_fusion.2 = f32[64,128,128]{2,1,0:T(8,128)} fusion(f32[64,128,128]{2,1,0:T(8,128)} %gather_fusion, pred[64]{0:T(512)(128)(4,1)S(1)} %get-tuple-element.235, f32[64,128,128]{2,1,0:T(8,128)} %gather_fusion.1, pred[64]{0:T(512)(128)(4,1)S(1)} %get-tuple-element.237, pred[64]{0:T(512)(128)(4,1)S(1)} %lt.176), kind=kOutput, calls=%fused_computation.7.clone.1 | convolution fusion | flops 1613758464 | bytes 12583104 | tf_op jit(solution)/shard_map/while/body/eval_jaxpr/pij,pjk->pik/dot_general | solution.py:46
  291.3 13.5 %scatter_fusion = f32[128,128,128]{2,1,0:T(8,128)} fusion(f32[128,128,128]{2,1,0:T(8,128)} %get-tuple-element.249, s32[64]{0:T(128)S(1)} %get-tuple-element.233, f32[64,128,128]{2,1,0:T(8,128)} %broadcast_select_fusion.2), kind=kCustom, calls=%fused_computation.2.clone.clone.1 | custom fusion | flops 1048576 | bytes 12583168 | tf_op jit(solution)/shard_map/while/body/eval_jaxpr/scatter-add | solution.py:48
  304.8 79.0 %reduce-scatter.2.cloned.1.call-done = f32[32,128,128]{2,1,0:T(8,128)} async-done(((f32[128,128,128]{2,1,0:T(8,128)}), f32[32,128,128]{2,1,0:T(8,128)}) %reduce-scatter.2.cloned.1.call-update) | async-done | bytes 2097168 | tf_op jit(solution)/shard_map/reduce_scatter | solution.py:92
  (151 shorter events, 6.2 us)
Async XLA Ops:
  6.5 46.3 %all-gather.2.cloned.1.call-start = ((), (), s32[]{:S(2)}) async-start(), calls=%async_computation.3 | async-start | bytes 2621440 | tf_op jit(solution)/shard_map/all_gather | solution.py:86
  21.3 31.5 %all-to-all-start.1 = ((f32[8,4,1,128,128]{4,3,1,2,0:T(8,128)}), f32[8,4,1,128,128]{4,3,1,2,0:T(8,128)S(1)}, u32[]{:S(2)}, u32[]{:S(2)}) async-start(f32[8,4,1,128,128]{4,3,1,2,0:T(8,128)} %broadcast_in_dim.74), calls=%async_computation.1 | async-start | bytes 4194304 | tf_op jit(solution)/shard_map/all_to_all | solution.py:29
  25.6 358.2 %reduce-scatter.2.cloned.1.call-start = ((), (), s32[]{:S(2)}) async-start(), calls=%async_computation.4 | async-start | bytes 10485760 | tf_op jit(solution)/shard_map/reduce_scatter | solution.py:92
  52.8 1.3 copy-start.1
  54.1 4.3 %copy-start = (f32[1,32,128,128]{3,2,0,1:T(8,128)S(1)}, f32[1,32,128,128]{3,2,0,1:T(8,128)}, u32[]{:S(2)}) copy-start(f32[1,32,128,128]{3,2,0,1:T(8,128)} %all-gather.2.cloned.1.call-done) | copy-start | bytes 6291460
Sparse Core Ops, SparseCore 0:
  9.0 33.4 all-gather.1
  304.9 78.8 reduce-scatter.1
where the time goes:
time: 393 us; the launch traced here: 391 us
  other arithmetic  109 us (28%)
  waiting for transfers between devices  105 us (27%)
  matrix products  80.5 us (20%)
  local copies, waits for them, and re-layouts  68.1 us (17%)
  between operations  13.5 us (3%)
  blocking collectives  9.69 us (2%)
  starting transfers between devices  4.34 us (1%)
    scatter-add x8, other arithmetic, add_pairs(): return totals.at[target].add(products)  107 us
    dot_general x8, matrix products, add_pairs(): jnp.einsum('pij,pjk->pik', lhs, rhs, precision=lax.Precision.HIGHEST)  80.5 us
    reduce_scatter x1, waiting for transfers between devices, per_device(): lax.psum_scatter(partial_value, 'layer', scatter_dimension=0, tiled=True)  79 us
    all_to_all x1, waiting for transfers between devices, copy_for_each(): return lax.all_to_all(copies, axis, split_axis=0, concat_axis=0, tiled=True)  25.4 us
    gather x8, local copies, waits for them, and re-layouts, add_pairs(): rhs = jnp.take(right_blocks, right_ids, axis=0)  22.1 us
    gather x8, local copies, waits for them, and re-layouts, add_pairs(): lhs = jnp.take(left_blocks, left_ids, axis=0)  22 us
    all_to_all x1, blocking collectives, side_by_side(): lax.all_to_all(both, axis, split_axis=split_dim, concat_axis=concat_dim,...  9.69 us
  transfers between devices with their start and end apart: 3, of which 2 were waited for; matrix products, arithmetic and copies ran while one was open for 2% of the time, Pallas kernels for 0%

commit v1 on v0

v1 whole, which is shorter than its diff:
```python
import jax
import jax.numpy as jnp
from jax import lax
from jax.experimental import pallas as pl
from jax.experimental.pallas import tpu as pltpu
from jax.sharding import PartitionSpec as P

BS = 128
ACAP = 8
BCAP = 4
PCAP = 16
CL = 32
N_ROW, N_COL, N_LAYER = 8, 4, 4
N_X = N_ROW // 2
A_ROWS = ACAP * BS
B_ROWS = BCAP * BS
Y_FIRST = 592
LISTS = N_ROW
PHASE = LISTS * PCAP
GROUP = 2
MESH = pl.DeviceIdType.MESH


def messages():
    out = {}

    def ring(tag, plus, minus, slot, rows, needs):
        start, stop = rows
        middle = (start + stop) // 2
        own = slot(0)
        up, down = tag + "+", tag + "-"
        out[up] = (plus, own, slot(3), rows, needs)
        out[down] = (minus, own, slot(1), rows, needs)
        out[up + "2"] = (plus, slot(3), slot(2), (start, middle), [up])
        out[down + "2"] = (minus, slot(1), slot(2), (middle, stop), [down])
        return {0: needs, 3: [up], 1: [down], 2: [up + "2", down + "2"]}

    first, second, whole = (0, Y_FIRST), (Y_FIRST, A_ROWS), (0, B_ROWS)
    by_layer = ring("By", "Y+", "Y-", lambda d: ("B", d, 0, 0), whole, [])
    a_layer = ring("Fy", "Y+", "Y-", lambda d: ("A", d, 0), first, [])
    a_col = ring("Gz", "Z+", "Z-", lambda e: ("A", 0, e), second, [])
    for d in (0, 3, 1, 2):
        ring(f"Bx{d}", "X+", "X-", lambda x: ("B", d, x, 0), whole, by_layer[d])
        ring(f"Fz{d}", "Z+", "Z-", lambda e: ("A", d, e), first, a_layer[d])
        ring(f"Gy{d}", "Y+", "Y-", lambda q: ("A", q, d), second, a_col[d])
    out["D"] = ("D", ("B", 0, 0, 0), ("B", 0, 0, 1), whole, [])
    for name in [n for n in out if n[0] == "B"]:
        _, _, target, rows, _ = out[name]
        out["D" + name] = ("D", target, target[:3] + (1,), rows, [name])
    return out


FIRST_SENDS = (
    "Gz+", "Gz-", "Fy+", "Fy-", "By+", "By-", "Bx0+", "Bx0-",
    "Fz0+", "Fz0-", "D", "Gy0+", "Gy0-",
)


def schedule():
    table = messages()
    row_time = {"D": 1.0}
    latency = {"D": 1100.0}
    ready_at, free_at, waited, started, steps = {}, {}, set(), set(), []
    now = 0.0

    def send(name):
        queue, _, _, (start, stop), _ = table[name]
        begin = max(now, free_at.get(queue, 0.0))
        free_at[queue] = begin + (stop - start) * row_time.get(queue, 11.0)
        ready_at[name] = free_at[queue] + latency.get(queue, 2000.0)
        started.add(name)
        steps.append(("send", name))

    for name in FIRST_SENDS:
        send(name)
    arrived_rows = {("A", 0, 0): A_ROWS, ("B", 0, 0, 0): B_ROWS}
    split, phases = set(), [(d, g) for d in (0, 3, 1, 2) for g in range(LISTS // GROUP)]
    slots = [("A", d, e) for d in range(4) for e in range(4)]
    slots += [("B", d, x, k) for d in range(4) for x in range(4) for k in range(2)]

    def task():
        if phases:
            d, g = phases[0]
            if all(s in split for s in slots if s[1] == d):
                phases.pop(0)
                return ("multiply", d, g), 420.0 * GROUP
        for s in sorted(slots, key=lambda s: ((0, 3, 1, 2).index(s[1]), s)):
            if s not in split and arrived_rows.get(s, 0) == (A_ROWS if s[0] == "A" else B_ROWS):
                split.add(s)
                return ("split", s), 300.0 if s[0] == "A" else 150.0
        return None

    while len(waited) < len(table) or phases:
        pending = sorted((ready_at[n], n) for n in started if n not in waited)
        if pending and pending[0][0] <= now:
            name = pending[0][1]
            waited.add(name)
            steps.append(("wait", name))
            target, (start, stop) = table[name][2], table[name][3]
            arrived_rows[target] = arrived_rows.get(target, 0) + stop - start
            for other, entry in table.items():
                if other not in started and all(n in waited for n in entry[4]):
                    send(other)
            continue
        chosen = task()
        if chosen is not None:
            steps.append(chosen[0])
            now += chosen[1]
        else:
            now = pending[0][0]
    return table, steps, now, free_at


def kernel(plan, a_ref, b_ref, out_ref, a_land, b_land, a_half, b_half, chain, send_sem, recv_sem):
    r, c, o = lax.axis_index("row"), lax.axis_index("col"), lax.axis_index("layer")
    devices = {
        "X+": (lax.rem(r + 2, N_ROW), c, o),
        "X-": (lax.rem(r + N_ROW - 2, N_ROW), c, o),
        "D": (r + 1 - 2 * lax.rem(r, 2), c, o),
        "Y+": (r, c, lax.rem(o + 1, N_LAYER)),
        "Y-": (r, c, lax.rem(o + N_LAYER - 1, N_LAYER)),
        "Z+": (r, lax.rem(c + 1, N_COL), o),
        "Z-": (r, lax.rem(c + N_COL - 1, N_COL), o),
    }
    table, steps, _, _ = schedule()

    def view(slot, rows):
        window = pl.ds(rows[0], rows[1] - rows[0])
        if slot == ("A", 0, 0):
            return a_ref.at[window]
        if slot == ("B", 0, 0, 0):
            return b_ref.at[window]
        if slot[0] == "A":
            return a_land.at[slot[1], slot[2], window]
        return b_land.at[slot[1], slot[2], slot[3], window]

    copies = {}
    for number, (name, (queue, source, target, rows, _)) in enumerate(table.items()):
        copies[name] = pltpu.make_async_remote_copy(
            src_ref=view(source, rows),
            dst_ref=view(target, rows),
            send_sem=send_sem.at[number],
            recv_sem=recv_sem.at[number],
            device_id=devices[queue],
            device_id_type=MESH,
        )

    barrier = pltpu.get_barrier_semaphore()
    for device in devices.values():
        pl.semaphore_signal(barrier, inc=1, device_id=device, device_id_type=MESH)
    pl.semaphore_wait(barrier, len(devices))

    def split(slot):
        if slot[0] == "A":
            base, blocks, halves = slot[2] * ACAP, ACAP, a_half
        else:
            base, blocks, halves = (slot[2] * 2 + slot[3]) * BCAP, BCAP, b_half
        source = view(slot, (0, blocks * BS))

        def one(block, carry):
            value = source[pl.ds(pl.multiple_of(block * BS, BS), BS), :]
            high = value.astype(jnp.bfloat16)
            low = (value - high.astype(jnp.float32)).astype(jnp.bfloat16)
            halves[slot[1], base + block, :, 0:BS] = high
            halves[slot[1], base + block, :, BS : 2 * BS] = low
            return carry

        lax.fori_loop(0, blocks, one, 0)

    def multiply(d, group):
        def one_list(index, carry):
            for p in range(PCAP):
                at = index * PCAP + p
                left = a_half[d, plan[d * PHASE + at]]
                right = b_half[d, plan[(4 + d) * PHASE + at]]
                both = jnp.dot(
                    left,
                    jnp.concatenate([right, right], axis=0),
                    preferred_element_type=jnp.float32,
                )
                before = chain[plan[(8 + d) * PHASE + at]]
                chain[at] = before + (both[:, 0:BS] + both[:, BS : 2 * BS])
            return carry

        lax.fori_loop(group * GROUP, (group + 1) * GROUP, one_list, 0)

    def collect(d, last):
        def one(t, carry):
            total = chain[plan[12 * PHASE + d * CL + t]]
            if last:
                out_ref[t] = total
            else:
                chain[PHASE + t] = total
            return carry

        lax.fori_loop(0, CL, one, 0)

    def clear(t, carry):
        chain[t] = jnp.zeros((BS, BS), jnp.float32)
        return carry

    cleared = False
    for step in steps:
        if step[0] == "send":
            copies[step[1]].start()
            continue
        if not cleared:
            lax.fori_loop(0, PHASE + CL, clear, 0)
            cleared = True
        if step[0] == "wait":
            copies[step[1]].wait_recv()
        elif step[0] == "split":
            split(step[1])
        else:
            _, d, group = step
            multiply(d, group)
            if group == LISTS // GROUP - 1:
                collect(d, d == 2)
    for copy in copies.values():
        copy.wait_send()


def tables(pair_plan, pair_counts):
    r, c, o = lax.axis_index("row"), lax.axis_index("col"), lax.axis_index("layer")
    phase = lax.rem(o + jnp.arange(N_LAYER, dtype=jnp.int32), N_LAYER)
    plan = jnp.take(pair_plan, phase, axis=1)
    counts = jnp.take(pair_counts, phase, axis=1)
    plan = jnp.moveaxis(plan, 0, 1)
    counts = jnp.moveaxis(counts, 0, 1)
    left, right, target = plan[:, :, 0], plan[:, :, 1], plan[:, :, 2]
    column = lax.rem(left // (N_LAYER * ACAP) + N_COL - c, N_COL)
    a_at = column * ACAP + left % ACAP
    s = jnp.arange(N_ROW, dtype=jnp.int32)
    x_on = lax.rem(s // 2 + N_X - r // 2, N_X)
    core_on = lax.rem(s + r, 2)
    b_at = ((x_on * 2 + core_on) * BCAP)[None, :, None] + right
    live = jnp.arange(PCAP, dtype=jnp.int32) < counts[:, :, None]
    key = jnp.where(live, target, -1).reshape(N_LAYER, PHASE)
    target = target.reshape(N_LAYER, PHASE)
    at = jnp.arange(PHASE, dtype=jnp.int32)
    earlier = (key[:, None, :] == target[:, :, None]) & (at[None, :] < at[:, None])
    previous = jnp.max(jnp.where(earlier, at, -1), axis=2)
    previous = jnp.where(previous < 0, PHASE + target, previous)
    result = jnp.arange(CL, dtype=jnp.int32)
    named = key[:, None, :] == result[:, None]
    last = jnp.max(jnp.where(named, at, -1), axis=2)
    last = jnp.where(last < 0, PHASE + result, last)
    parts = [a_at.reshape(-1), b_at.reshape(-1), previous.reshape(-1), last.reshape(-1)]
    return jnp.concatenate(parts)


def per_device(a_blocks, b_blocks, pair_plan, pair_counts):
    plan = tables(pair_plan[0, 0, 0], pair_counts[0, 0, 0])
    count = len(messages())
    vmem = pl.BlockSpec(memory_space=pltpu.VMEM)
    result = pl.pallas_call(
        kernel,
        out_shape=jax.ShapeDtypeStruct((CL, BS, BS), jnp.float32),
        in_specs=[pl.BlockSpec(memory_space=pltpu.SMEM), vmem, vmem],
        out_specs=vmem,
        scratch_shapes=[
            pltpu.VMEM((N_LAYER, N_COL, A_ROWS, BS), jnp.float32),
            pltpu.VMEM((N_LAYER, N_X, 2, B_ROWS, BS), jnp.float32),
            pltpu.VMEM((N_LAYER, N_COL * ACAP, BS, 2 * BS), jnp.bfloat16),
            pltpu.VMEM((N_LAYER, N_ROW * BCAP, BS, 2 * BS), jnp.bfloat16),
            pltpu.VMEM((PHASE + CL, BS, BS), jnp.float32),
            pltpu.SemaphoreType.DMA((count,)),
            pltpu.SemaphoreType.DMA((count,)),
        ],
        compiler_params=pltpu.CompilerParams(
            collective_id=0, has_side_effects=True, vmem_limit_bytes=60 * 1024 * 1024
        ),
        name="gather_multiply",
    )(plan, a_blocks.reshape(A_ROWS, BS), b_blocks.reshape(B_ROWS, BS))
    return result[None, None]


def solution(mesh):
    in_specs = (
        P("row", ("col", "layer"), None, None),
        P(("row", "layer"), "col", None, None),
        P("row", "col", "layer", None, None, None, None),
        P("row", "col", "layer", None, None),
    )
    out_specs = P("row", "col", "layer", None, None)
    return jax.shard_map(
        per_device, mesh=mesh, in_specs=in_specs, out_specs=out_specs, check_vma=False
    )
```

time: 393 us -> 75.6 us (0.19)
  other arithmetic: 109 us -> 1.28 us
  waiting for transfers between devices: 105 us -> 0 us
  matrix products: 80.5 us -> 0 us
  Pallas kernels: 0 us -> 67.4 us
  local copies, waits for them, and re-layouts: 68.1 us -> 6.59 us
  between operations: 13.5 us -> 0.07 us
  blocking collectives: 9.69 us -> 0 us
  starting transfers between devices: 4.34 us -> 0 us
    scatter-add x8 -> x0, other arithmetic: 107 us -> none  [add_pairs(): return totals.at[target].add(products)]
    dot_general x8 -> x0, matrix products: 80.5 us -> none  [add_pairs(): jnp.einsum('pij,pjk->pik', lhs, rhs, precision=lax.Precision.HIGHEST)]
    reduce_scatter x1 -> x0, waiting for transfers between devices: 79 us -> none  [per_device(): lax.psum_scatter(partial_value, 'layer', scatter_dimension=0, tiled=True)]
    pallas_call x0 -> x1, Pallas kernels: none -> 67.4 us  [per_device(): pl.pallas_call(kernel, out_shape=jax.ShapeDtypeStruct((CL, BS, BS), jnp.f...]
    gather x16 -> x2, local copies, waits for them, and re-layouts: 44.1 us -> 1.11 us  [the longest x1 0.56 us: tables(): counts = jnp.take(pair_counts, phase, axis=1)]
    all_to_all x1 -> x0, waiting for transfers between devices: 25.4 us -> none  [copy_for_each(): return lax.all_to_all(copies, axis, split_axis=0, concat_axis=0, tiled=True)]
    squeeze x56 -> x3, local copies, waits for them, and re-layouts: 11.1 us -> 0.24 us  [tables(): left, right, target = (plan[:, :, 0], plan[:, :, 1], plan[:, :, 2])]
    all_to_all x1 -> x0, blocking collectives: 9.69 us -> none  [side_by_side(): lax.all_to_all(both, axis, split_axis=split_dim, concat_axis=concat_dim,...]
  transfers between devices with their start and end apart: 3 -> 0, of which waited for: 2 -> 0; matrix products, arithmetic and copies ran while one was open for 2% -> 0% of each run, Pallas kernels for 0% -> 0%
where the time goes in v1:
time: 75.6 us; the launch traced here: 75.4 us
  Pallas kernels  67.4 us (89%)
  local copies, waits for them, and re-layouts  6.59 us (9%)
  other arithmetic  1.28 us (2%)
    pallas_call x1, Pallas kernels, per_device(): pl.pallas_call(kernel, out_shape=jax.ShapeDtypeStruct((CL, BS, BS), jnp.f...  67.4 us
    unnamed x4, local copies, waits for them, and re-layouts  4.61 us

profile of v1, /device:TPU:0, one launch (start us, length us, event | category | flops | bytes accessed | tf_op | source)
XLA Modules:
  0.0 75.4 jit_solution(10604272086519509946)
XLA Ops:
  0.0 0.0 copy-start
  0.0 0.7 copy-done
  0.7 0.1 broadcast_in_dim.65
  0.8 0.6 gather_fusion.1
  1.4 0.1 broadcast_select_fusion.1
  1.5 0.1 lt.79
  1.5 0.1 lt.81
  1.6 0.1 lt.82
  1.7 0.1 add.123
  1.8 0.1 add.124
  1.9 0.8 %copy.8 = s32[1,1,1,8,4,3,16]{6,3,5,4,2,1,0:T(8,128)S(1)} copy(s32[1,1,1,8,4,3,16]{6,4,5,3,2,1,0:T(4,128)} %param.6) | data formatting | bytes 12288 | tf_op args[2]
  2.7 0.6 gather_fusion
  3.2 0.1 broadcast_select_fusion
  3.3 0.1 squeeze.16
  3.4 0.1 squeeze.19
  3.5 0.3 select_reduce_fusion
  3.7 0.1 select_reduce_fusion.1
  3.9 0.1 reduce_max.25
  4.0 0.1 add.128
  4.1 0.1 squeeze.17
  4.2 0.6 pad_add_fusion.plan
  4.8 67.4 %gather_multiply.1 = f32[32,128,128]{2,1,0:T(8,128)} custom-call(s32[1664]{0:T(1024)} %pad_add_fusion.plan, f32[1024,128]{1,0:T(8,128)} %bitcast.29, f32[512,128]{1,0:T(8,128)} %bitcast.31), custom_call_target="tpu_custom_call" | custom-call | tf_op jit(solution)/shard_map/gather_multiply/pallas_call | solution.py:256
  72.2 3.1 %copy.10 = f32[1,1,32,128,128]{4,3,2,1,0:T(8,128)} copy(f32[1,1,32,128,128]{4,3,2,1,0:T(8,128)} %bitcast.28) | data formatting | bytes 4194304
  (13 shorter events, 0.1 us)
Async XLA Ops:
  0.0 0.7 copy-start

commit v2 on v0

v2 whole, which is shorter than its diff:
```python
import jax
import jax.numpy as jnp
from jax import lax
from jax.experimental import pallas as pl
from jax.experimental.pallas import tpu as pltpu
from jax.sharding import PartitionSpec as P

BS = 128
ACAP = 8
BCAP = 4
PCAP = 16
CL = 32
N_ROW, N_COL, N_LAYER = 8, 4, 4
N_X = N_ROW // 2
LISTS = N_ROW
PHASE = LISTS * PCAP
GROUPS = 2
UNROLL = 64
ORDER = (0, 3, 1, 2)
MESH = pl.DeviceIdType.MESH


def messages():
    out = {}

    def put(name, *entry):
        out[name] = entry

    put("Fy+", "Y+", ("A", 0, 0), ("A", 3, 0), (0, 6), [])
    put("Fy-", "Y-", ("A", 0, 0), ("A", 1, 0), (4, 8), [])
    put("Hy+", "Y+", ("A", 0, 0), ("A", 3, 0), (6, 8), [])
    put("Hy-", "Y-", ("A", 0, 0), ("A", 1, 0), (0, 4), [])
    put("Fy+2", "Y+", ("A", 3, 0), ("A", 2, 0), (0, 4), ["Fy+"])
    put("Fy-2", "Y-", ("A", 1, 0), ("A", 2, 0), (4, 8), ["Fy-"])
    put("Gz+", "Z+", ("A", 0, 0), ("A", 0, 3), (0, 4), [])
    put("Gz-", "Z-", ("A", 0, 0), ("A", 0, 1), (4, 8), [])
    put("Iz+", "Z+", ("A", 0, 0), ("A", 0, 3), (4, 8), [])
    put("Iz-", "Z-", ("A", 0, 0), ("A", 0, 1), (0, 4), [])
    put("Gz+2", "Z+", ("A", 0, 3), ("A", 0, 2), (0, 4), ["Gz+"])
    put("Gz-2", "Z-", ("A", 0, 1), ("A", 0, 2), (4, 8), ["Gz-"])
    put("Fz3+", "Z+", ("A", 3, 0), ("A", 3, 3), (0, 3), ["Fy+"])
    put("Fz3-", "Z-", ("A", 3, 0), ("A", 3, 1), (3, 6), ["Fy+"])
    put("Iz3+", "Z+", ("A", 3, 0), ("A", 3, 3), (3, 6), ["Fy+"])
    put("Iz3-", "Z-", ("A", 3, 0), ("A", 3, 1), (0, 3), ["Fy+"])
    put("Fz3+2", "Z+", ("A", 3, 3), ("A", 3, 2), (0, 3), ["Fz3+"])
    put("Fz3-2", "Z-", ("A", 3, 1), ("A", 3, 2), (3, 6), ["Fz3-"])
    put("Fz1+", "Z+", ("A", 1, 0), ("A", 1, 3), (4, 6), ["Fy-"])
    put("Fz1-", "Z-", ("A", 1, 0), ("A", 1, 1), (6, 8), ["Fy-"])
    put("Iz1+", "Z+", ("A", 1, 0), ("A", 1, 3), (6, 8), ["Fy-"])
    put("Iz1-", "Z-", ("A", 1, 0), ("A", 1, 1), (4, 6), ["Fy-"])
    put("Fz1+2", "Z+", ("A", 1, 3), ("A", 1, 2), (4, 6), ["Fz1+"])
    put("Fz1-2", "Z-", ("A", 1, 1), ("A", 1, 2), (6, 8), ["Fz1-"])
    upper = {3: ["Iz+"], 1: ["Gz-"], 2: ["Gz-2"]}
    lower = {3: ["Gz+"], 1: ["Iz-"], 2: ["Gz+2"]}
    for e in (3, 1, 2):
        put(f"Gy{e}+", "Y+", ("A", 0, e), ("A", 3, e), (6, 8), upper[e])
        put(f"Gy{e}-", "Y-", ("A", 0, e), ("A", 1, e), (0, 4), lower[e])
    fifth = {3: ["Iz3+"], 1: ["Fz3-"], 2: ["Fz3-2"]}
    fourth = {3: ["Fz1+"], 1: ["Iz1-"], 2: ["Fz1+2"]}
    for e in (3, 1, 2):
        put(f"Gy{e}+2", "Y+", ("A", 3, e), ("A", 2, e), (5, 8), [f"Gy{e}+"] + fifth[e])
        put(f"Gy{e}-2", "Y-", ("A", 1, e), ("A", 2, e), (4, 5), fourth[e])
    put("Fz2+", "Z+", ("A", 2, 0), ("A", 2, 3), (0, 2), ["Fy+2"])
    put("Fz2-", "Z-", ("A", 2, 0), ("A", 2, 1), (2, 4), ["Fy+2"])
    put("Iz2+", "Z+", ("A", 2, 0), ("A", 2, 3), (2, 4), ["Fy+2"])
    put("Iz2-", "Z-", ("A", 2, 0), ("A", 2, 1), (0, 2), ["Fy+2"])
    put("Fz2+2", "Z+", ("A", 2, 3), ("A", 2, 2), (0, 2), ["Fz2+"])
    put("Fz2-2", "Z-", ("A", 2, 1), ("A", 2, 2), (2, 4), ["Fz2-"])
    put("By+", "Y+", ("B", 0, 0, 0), ("B", 3, 0, 0), (0, 4), [])
    put("By-", "Y-", ("B", 0, 0, 0), ("B", 1, 0, 0), (0, 4), [])
    put("By+2", "Y+", ("B", 3, 0, 0), ("B", 2, 0, 0), (0, 2), ["By+"])
    put("By-2", "Y-", ("B", 1, 0, 0), ("B", 2, 0, 0), (2, 4), ["By-"])
    layer = {0: [], 3: ["By+"], 1: ["By-"], 2: ["By+2", "By-2"]}
    for d in ORDER:
        put(f"Bx{d}+", "X+", ("B", d, 0, 0), ("B", d, 3, 0), (0, 4), layer[d])
        put(f"Bx{d}-", "X-", ("B", d, 0, 0), ("B", d, 1, 0), (0, 4), layer[d])
        put(f"Bx{d}+2", "X+", ("B", d, 3, 0), ("B", d, 2, 0), (0, 2), [f"Bx{d}+"])
        put(f"Bx{d}-2", "X-", ("B", d, 1, 0), ("B", d, 2, 0), (2, 4), [f"Bx{d}-"])
        sources = {0: layer[d], 3: [f"Bx{d}+"], 1: [f"Bx{d}-"], 2: [f"Bx{d}+2", f"Bx{d}-2"]}
        for x, needs in sources.items():
            put(f"D{d}{x}", "D", ("B", d, x, 0), ("B", d, x, 1), (0, 4), needs)
    return out


Z_ORDER = (
    "Gz*", "Iz*", "Gz*2", "Fz3*", "Iz3*", "Fz3*2", "Fz1*", "Iz1*", "Fz1*2", "Fz2*", "Iz2*", "Fz2*2",
)
Y_ORDER = (
    "By*", "Fy*", "Hy*", "By*2", "Gy3*", "Gy1*", "Gy2*", "Fy*2", "Gy3*2", "Gy1*2", "Gy2*2",
)
X_ORDER = ("Bx0*", "Bx0*2", "Bx3*", "Bx1*", "Bx3*2", "Bx1*2", "Bx2*", "Bx2*2")


AFTER = {0: ("Gz+2", "Gz-2"), 3: ("Fz1+", "Fz1-"), 1: ("Fz2+", "Fz2-"), 2: ()}


def groups():
    out = {"By2": ("By+2", "By-2"), "Gy+": ("Gy3+", "Gy1+", "Gy2+"), "Gy-": ("Gy3-", "Gy1-", "Gy2-")}
    for d in ORDER:
        out[f"Bx{d}2"] = (f"Bx{d}+2", f"Bx{d}-2")
        out[f"D{d}"] = tuple(f"D{d}{x}" for x in range(N_X))
    grouped = {n for names in out.values() for n in names}
    out.update({n: (n,) for n in messages() if n not in grouped})
    return out


def schedule():
    table = messages()
    ready_at, free_at, waited, started, steps = {}, {}, set(), set(), []
    now = 0.0

    def send(name):
        queue, _, _, blocks, _ = table[name]
        begin = max(now, free_at.get(queue, 0.0))
        free_at[queue] = begin + (blocks[1] - blocks[0]) * (128.0 if queue == "D" else 1420.0)
        ready_at[name] = free_at[queue] + (1100.0 if queue == "D" else 2400.0)
        started.add(name)
        steps.append(("send", name))

    order = {
        axis + sign: [n.replace("*", sign) for n in names]
        for axis, names in (("Z", Z_ORDER), ("Y", Y_ORDER), ("X", X_ORDER))
        for sign in "+-"
    }

    def send_ready():
        for names in order.values():
            while names and all(n in waited for n in table[names[0]][4]):
                send(names.pop(0))
        for name, entry in table.items():
            if entry[0] == "D" and name not in started and all(n in waited for n in entry[4]):
                send(name)

    send_ready()
    steps.append(("tables",))
    now += 2500.0
    ripe = [(("A", 0, 0), (0, ACAP)), (("B", 0, 0, 0), (0, BCAP))]
    missing = {d: N_COL * ACAP + N_ROW * BCAP for d in ORDER}
    phases = [(d, g) for d in ORDER for g in range(GROUPS)]
    together = groups()

    def task():
        if phases and missing[phases[0][0]] == 0 and all(n in waited for n in AFTER[phases[0][0]]):
            d, g = phases.pop(0)
            return ("multiply", d, g), 2500.0 / GROUPS + (400.0 if g == GROUPS - 1 else 0.0)
        if ripe:
            slot, blocks = ripe.pop(min(range(len(ripe)), key=lambda i: ORDER.index(ripe[i][0][1])))
            missing[slot[1]] -= blocks[1] - blocks[0]
            return ("split", slot, blocks), 35.0 * (blocks[1] - blocks[0]) + 30.0
        return None

    while len(waited) < len(table) or phases:
        pending = sorted(
            (max(ready_at[n] for n in names), group)
            for group, names in together.items()
            if all(n in started for n in names) and names[0] not in waited
        )
        if pending and pending[0][0] <= now:
            group = pending[0][1]
            waited.update(together[group])
            steps.append(("wait", group))
            ripe.extend(table[n][2:4] for n in together[group])
            send_ready()
            continue
        chosen = task()
        if chosen is not None:
            steps.append(chosen[0])
            now += chosen[1]
        else:
            now = pending[0][0]
    return table, steps, now, free_at


def kernel(
    a_ref, b_ref, plan_ref, counts_ref, out_ref,
    a_land, b_land, a_half, b_half, chain, sums, plan_v, counts_v, table_v, table_s, own_sem, send_sem, recv_sem,
):
    r, c, o = lax.axis_index("row"), lax.axis_index("col"), lax.axis_index("layer")
    devices = {
        "X+": (lax.rem(r + 2, N_ROW), c, o),
        "X-": (lax.rem(r + N_ROW - 2, N_ROW), c, o),
        "D": (r + 1 - 2 * lax.rem(r, 2), c, o),
        "Y+": (r, c, lax.rem(o + 1, N_LAYER)),
        "Y-": (r, c, lax.rem(o + N_LAYER - 1, N_LAYER)),
        "Z+": (r, lax.rem(c + 1, N_COL), o),
        "Z-": (r, lax.rem(c + N_COL - 1, N_COL), o),
    }
    own = [
        pltpu.make_async_copy(a_ref, a_land.at[0, 0], own_sem.at[0]),
        pltpu.make_async_copy(b_ref, b_land.at[0, 0, 0], own_sem.at[1]),
        pltpu.make_async_copy(plan_ref, plan_v, own_sem.at[2]),
        pltpu.make_async_copy(counts_ref, counts_v, own_sem.at[3]),
    ]
    to_scalar = pltpu.make_async_copy(table_v, table_s, own_sem.at[4])
    for copy in own:
        copy.start()
    barrier = pltpu.get_barrier_semaphore()
    for device in devices.values():
        pl.semaphore_signal(barrier, inc=1, device_id=device, device_id_type=MESH)
    pl.semaphore_wait(barrier, len(devices))
    own[0].wait()
    own[1].wait()

    table, steps, _, _ = schedule()

    def view(slot, blocks):
        land = a_land if slot[0] == "A" else b_land
        return land.at[(*slot[1:], pl.ds(blocks[0], blocks[1] - blocks[0]))]

    together = groups()
    number = {n: i for i, names in enumerate(together.values()) for n in names}
    copies, sent, size = {}, [0, 0], [0] * len(together)
    for name, (queue, source, target, blocks, _) in table.items():
        pool = 0 if queue[0] in "YZ" else 1
        sent[pool] += blocks[1] - blocks[0]
        size[number[name]] += blocks[1] - blocks[0]
        copies[name] = pltpu.make_async_remote_copy(
            src_ref=view(source, blocks),
            dst_ref=view(target, blocks),
            send_sem=send_sem.at[pool],
            recv_sem=recv_sem.at[number[name]],
            device_id=devices[queue],
            device_id_type=MESH,
        )

    def make_tables():
        own[2].wait()
        own[3].wait()
        shape = (N_LAYER, PHASE)
        fields = [
            jnp.concatenate([plan_v[s, f] for s in range(LISTS)], axis=1) for f in range(3)
        ]
        limit = jnp.concatenate(
            [jnp.broadcast_to(counts_v[:, s : s + 1], (N_LAYER, PCAP)) for s in range(LISTS)], axis=1
        )
        left, right, target = fields
        at = lax.broadcasted_iota(jnp.int32, shape, 1)
        s = at // PCAP
        column = (left // (N_LAYER * ACAP) + N_COL - c) % N_COL
        x_on = (s // 2 + N_X - r // 2) % N_X
        core_on = (s + r) % 2
        live = at % PCAP < limit
        key = jnp.where(live, target, CL) * PHASE + at
        packed = (target * PHASE + column * ACAP + left % ACAP) * PHASE
        packed = packed + (x_on * 2 + core_on) * BCAP + right
        rank = jnp.zeros(shape, jnp.int32)
        for q in range(PHASE):
            rank += jnp.where(jnp.broadcast_to(key[:, q : q + 1], shape) < key, 1, 0)
        ordered, place, last = packed, target, jnp.full(shape, -1, jnp.int32)
        sort_key = key // PHASE
        for q in range(PHASE):
            here = at == jnp.broadcast_to(rank[:, q : q + 1], shape)
            ordered = jnp.where(here, jnp.broadcast_to(packed[:, q : q + 1], shape), ordered)
            place = jnp.where(here, jnp.broadcast_to(sort_key[:, q : q + 1], shape), place)
            one = jnp.broadcast_to(sort_key[:, q : q + 1], shape)
            last = jnp.where(at == one, jnp.maximum(last, jnp.broadcast_to(rank[:, q : q + 1], shape)), last)
        earlier = jnp.concatenate([place[:, 0:1] - 1, place[:, 0 : PHASE - 1]], axis=1)
        table_v[0:4] = ordered // PHASE % PHASE
        table_v[4:8] = ordered % PHASE
        table_v[8:12] = ordered // (PHASE * PHASE)
        table_v[12:16] = jnp.where(place == earlier, 0, 1)
        table_v[16:20] = jnp.where(last < 0, PHASE + at, last)

    def wait_for(sem, blocks):
        window = chain.at[pl.ds(0, blocks)]
        pltpu.make_async_copy(window, window, sem).wait()

    def split(slot, blocks):
        if slot[0] == "A":
            base, halves, land = slot[2] * ACAP, a_half, a_land
        else:
            base, halves, land = (slot[2] * 2 + slot[3]) * BCAP, b_half, b_land

        def one(block, carry):
            value = land[(*slot[1:], block)]
            high = value.astype(jnp.bfloat16)
            low = (value - high.astype(jnp.float32)).astype(jnp.bfloat16)
            halves[slot[1], base + block, :, 0:BS] = high
            halves[slot[1], base + block, :, BS : 2 * BS] = low
            return carry

        lax.fori_loop(*blocks, one, 0)

    def multiply(d, total, group):
        m = lax.rem(o + d, N_LAYER)
        steps_of_group = PHASE // GROUPS // UNROLL

        def some(index, total):
            for p in range(UNROLL):
                at = index * UNROLL + p
                left = a_half[d, table_s[m, at]]
                right = b_half[d, table_s[4 + m, at]]
                both = jnp.dot(
                    left,
                    jnp.concatenate([right, right], axis=0),
                    preferred_element_type=jnp.float32,
                )
                first = jnp.broadcast_to(table_s[12 + m, at], (BS, BS)) == 1
                total = jnp.where(first, sums[table_s[8 + m, at]], total)
                total = total + (both[:, 0:BS] + both[:, BS : 2 * BS])
                chain[at] = total
            return total

        return lax.fori_loop(group * steps_of_group, (group + 1) * steps_of_group, some, total)

    def collect(d):
        m = lax.rem(o + d, N_LAYER)

        def one(t, carry):
            at = table_s[16 + m, t]
            total = jnp.where(
                jnp.broadcast_to(at, (BS, BS)) < PHASE, chain[jnp.minimum(at, PHASE - 1)], sums[t]
            )
            if d == ORDER[-1]:
                out_ref[t] = total
            else:
                sums[t] = total
            return carry

        lax.fori_loop(0, CL, one, 0)

    def clear(t, carry):
        sums[t] = jnp.zeros((BS, BS), jnp.float32)
        return carry

    scalars, running = "none", jnp.zeros((BS, BS), jnp.float32)
    for step in steps:
        if step[0] == "send":
            copies[step[1]].start()
        elif step[0] == "tables":
            make_tables()
            lax.fori_loop(0, CL, clear, 0)
        elif step[0] == "wait":
            names = together[step[1]]
            if len(names) == 1:
                copies[names[0]].wait_recv()
            else:
                wait_for(recv_sem.at[number[names[0]]], size[number[names[0]]])
            if scalars == "none":
                to_scalar.start()
                scalars = "started"
        elif step[0] == "split":
            split(*step[1:])
        else:
            if scalars == "started":
                to_scalar.wait()
                scalars = "there"
            running = multiply(step[1], running, step[2])
            if step[2] == GROUPS - 1:
                collect(step[1])
    for pool in range(2):
        wait_for(send_sem.at[pool], sent[pool])


def per_device(a_blocks, b_blocks, pair_plan, pair_counts):
    count = len(groups())
    hbm = pl.BlockSpec(memory_space=pltpu.HBM)
    plan = pair_plan[0, 0, 0].transpose(0, 2, 1, 3)
    operands = (a_blocks[0], b_blocks[:, 0], plan, pair_counts[0, 0, 0].T)
    result = pl.pallas_call(
        kernel,
        out_shape=jax.ShapeDtypeStruct((CL, BS, BS), jnp.float32),
        in_specs=[hbm, hbm, hbm, hbm],
        out_specs=pl.BlockSpec(memory_space=pltpu.VMEM),
        scratch_shapes=[
            pltpu.VMEM((N_LAYER, N_COL, ACAP, BS, BS), jnp.float32),
            pltpu.VMEM((N_LAYER, N_X, 2, BCAP, BS, BS), jnp.float32),
            pltpu.VMEM((N_LAYER, N_COL * ACAP, BS, 2 * BS), jnp.bfloat16),
            pltpu.VMEM((N_LAYER, N_ROW * BCAP, BS, 2 * BS), jnp.bfloat16),
            pltpu.VMEM((PHASE + BCAP, BS, BS), jnp.float32),
            pltpu.VMEM((CL, BS, BS), jnp.float32),
            pltpu.VMEM((N_ROW, 3, N_LAYER, PCAP), jnp.int32),
            pltpu.VMEM((N_LAYER, N_ROW), jnp.int32),
            pltpu.VMEM((24, PHASE), jnp.int32),
            pltpu.SMEM((24, PHASE), jnp.int32),
            pltpu.SemaphoreType.DMA((5,)),
            pltpu.SemaphoreType.DMA((2,)),
            pltpu.SemaphoreType.DMA((count,)),
        ],
        compiler_params=pltpu.CompilerParams(
            collective_id=0, has_side_effects=True, vmem_limit_bytes=50 * 1024 * 1024
        ),
        name="gather_multiply",
    )(*[pltpu.with_memory_space_constraint(x, pltpu.HBM) for x in operands])
    return result[None, None]


def solution(mesh):
    in_specs = (
        P("row", ("col", "layer"), None, None),
        P(("row", "layer"), "col", None, None),
        P("row", "col", "layer", None, None, None, None),
        P("row", "col", "layer", None, None),
    )
    out_specs = P("row", "col", "layer", None, None)
    return jax.shard_map(
        per_device, mesh=mesh, in_specs=in_specs, out_specs=out_specs, check_vma=False
    )
```

time: 393 us -> 60 us (0.15)
  other arithmetic: 109 us -> 0 us
  waiting for transfers between devices: 105 us -> 0 us
  matrix products: 80.5 us -> 0 us
  local copies, waits for them, and re-layouts: 68.1 us -> 1.32 us
  Pallas kernels: 0 us -> 57.5 us
  between operations: 13.5 us -> 0.01 us
  blocking collectives: 9.69 us -> 0 us
  starting transfers between devices: 4.34 us -> 0 us
    scatter-add x8 -> x0, other arithmetic: 107 us -> none  [add_pairs(): return totals.at[target].add(products)]
    dot_general x8 -> x0, matrix products: 80.5 us -> none  [add_pairs(): jnp.einsum('pij,pjk->pik', lhs, rhs, precision=lax.Precision.HIGHEST)]
    reduce_scatter x1 -> x0, waiting for transfers between devices: 79 us -> none  [per_device(): lax.psum_scatter(partial_value, 'layer', scatter_dimension=0, tiled=True)]
    pallas_call x0 -> x1, Pallas kernels: none -> 57.5 us  [per_device(): pl.pallas_call(kernel, out_shape=jax.ShapeDtypeStruct((CL, BS, BS), jnp.f...]
    gather x16 -> x0, local copies, waits for them, and re-layouts: 44.1 us -> none  [the longest x8 22.1 us: add_pairs(): rhs = jnp.take(right_blocks, right_ids, axis=0)]
    all_to_all x1 -> x0, waiting for transfers between devices: 25.4 us -> none  [copy_for_each(): return lax.all_to_all(copies, axis, split_axis=0, concat_axis=0, tiled=True)]
    squeeze x56 -> x0, local copies, waits for them, and re-layouts: 11.1 us -> none  [the longest x8 7.79 us: per_shard(): blocks = lax.dynamic_slice_in_dim(piece, index * BCAP, BCAP, 0)[:, 0]]
    all_to_all x1 -> x0, blocking collectives: 9.69 us -> none  [side_by_side(): lax.all_to_all(both, axis, split_axis=split_dim, concat_axis=concat_dim,...]
  transfers between devices with their start and end apart: 3 -> 0, of which waited for: 2 -> 0; matrix products, arithmetic and copies ran while one was open for 2% -> 0% of each run, Pallas kernels for 0% -> 0%
where the time goes in v2:
time: 60 us; the launch traced here: 58.8 us
  Pallas kernels  57.5 us (96%)
  local copies, waits for them, and re-layouts  1.32 us (2%)
    pallas_call x1, Pallas kernels, per_device(): pl.pallas_call(kernel, out_shape=jax.ShapeDtypeStruct((CL, BS, BS), jnp.f...  57.5 us
    unnamed x1, local copies, waits for them, and re-layouts  1.32 us

profile of v2, /device:TPU:0, one launch (start us, length us, event | category | flops | bytes accessed | tf_op | source)
XLA Modules:
  0.0 58.8 jit_solution(3783197198984518752)
XLA Ops:
  0.0 57.5 %gather_multiply.1 = f32[32,128,128]{2,1,0:T(8,128)S(1)} custom-call(f32[8,128,128]{2,1,0:T(8,128)} %bitcast.10, f32[4,128,128]{2,1,0:T(8,128)} %bitcast.11, s32[8,3,4,16]{3,2,1,0:T(4,128)} %bitcast.12, s32[4,8]{1,0:T(4,128)} %bitcast.13), custom_call_target="tpu_custom_call" | custom-call | tf_op jit(solution)/shard_map/gather_multiply/pallas_call | solution.py:360
  57.5 1.3 %copy.6 = f32[1,1,32,128,128]{4,3,2,1,0:T(8,128)} copy(f32[1,1,32,128,128]{4,3,2,1,0:T(8,128)S(1)} %bitcast.9) | data formatting | bytes 4194304

commit v3 on v2

--- a/solution.py
+++ b/solution.py
@@ -14,8 +14,7 @@
 N_X = N_ROW // 2
 LISTS = N_ROW
 PHASE = LISTS * PCAP
-GROUPS = 2
-UNROLL = 64
+UNROLL = {0: 32, 3: 32, 1: 32, 2: 128}
 ORDER = (0, 3, 1, 2)
 MESH = pl.DeviceIdType.MESH
 
@@ -136,13 +135,12 @@
     now += 2500.0
     ripe = [(("A", 0, 0), (0, ACAP)), (("B", 0, 0, 0), (0, BCAP))]
     missing = {d: N_COL * ACAP + N_ROW * BCAP for d in ORDER}
-    phases = [(d, g) for d in ORDER for g in range(GROUPS)]
+    phases = list(ORDER)
     together = groups()
 
     def task():
-        if phases and missing[phases[0][0]] == 0 and all(n in waited for n in AFTER[phases[0][0]]):
-            d, g = phases.pop(0)
-            return ("multiply", d, g), 2500.0 / GROUPS + (400.0 if g == GROUPS - 1 else 0.0)
+        if phases and missing[phases[0]] == 0 and all(n in waited for n in AFTER[phases[0]]):
+            return ("multiply", phases.pop(0)), 2900.0
         if ripe:
             slot, blocks = ripe.pop(min(range(len(ripe)), key=lambda i: ORDER.index(ripe[i][0][1])))
             missing[slot[1]] -= blocks[1] - blocks[0]
@@ -281,13 +279,13 @@
 
         lax.fori_loop(*blocks, one, 0)
 
-    def multiply(d, total, group):
+    def multiply(d, total):
         m = lax.rem(o + d, N_LAYER)
-        steps_of_group = PHASE // GROUPS // UNROLL
+        unroll = UNROLL[d]
 
         def some(index, total):
-            for p in range(UNROLL):
-                at = index * UNROLL + p
+            for p in range(unroll):
+                at = index * unroll + p
                 left = a_half[d, table_s[m, at]]
                 right = b_half[d, table_s[4 + m, at]]
                 both = jnp.dot(
@@ -301,7 +299,7 @@
                 chain[at] = total
             return total
 
-        return lax.fori_loop(group * steps_of_group, (group + 1) * steps_of_group, some, total)
+        return lax.fori_loop(0, PHASE // unroll, some, total)
 
     def collect(d):
         m = lax.rem(o + d, N_LAYER)
@@ -345,9 +343,8 @@
             if scalars == "started":
                 to_scalar.wait()
                 scalars = "there"
-            running = multiply(step[1], running, step[2])
-            if step[2] == GROUPS - 1:
-                collect(step[1])
+            running = multiply(step[1], running)
+            collect(step[1])
     for pool in range(2):
         wait_for(send_sem.at[pool], sent[pool])
 

time: 60 us -> 59 us (0.983); the launches traced: 58.8 us -> 58.9 us
  no operation moved by 1% of the time
where the time goes in v3:
time: 59 us; the launch traced here: 58.9 us
  Pallas kernels  57.5 us (97%)
  local copies, waits for them, and re-layouts  1.32 us (2%)
    pallas_call x1, Pallas kernels, per_device(): pl.pallas_call(kernel, out_shape=jax.ShapeDtypeStruct((CL, BS, BS), jnp.f...  57.5 us
    unnamed x1, local copies, waits for them, and re-layouts  1.32 us

profile of v3, /device:TPU:0, one launch (start us, length us, event | category | flops | bytes accessed | tf_op | source)
XLA Modules:
  0.0 58.9 jit_solution(2337312558261654764)
XLA Ops:
  0.0 57.5 %gather_multiply.1 = f32[32,128,128]{2,1,0:T(8,128)S(1)} custom-call(f32[8,128,128]{2,1,0:T(8,128)} %bitcast.10, f32[4,128,128]{2,1,0:T(8,128)} %bitcast.11, s32[8,3,4,16]{3,2,1,0:T(4,128)} %bitcast.12, s32[4,8]{1,0:T(4,128)} %bitcast.13), custom_call_target="tpu_custom_call" | custom-call | tf_op jit(solution)/shard_map/gather_multiply/pallas_call | solution.py:357
  57.5 1.3 %copy.6 = f32[1,1,32,128,128]{4,3,2,1,0:T(8,128)} copy(f32[1,1,32,128,128]{4,3,2,1,0:T(8,128)S(1)} %bitcast.9) | data formatting | bytes 4194304

commit v4 on v3

--- a/solution.py
+++ b/solution.py
@@ -269,15 +269,22 @@
         else:
             base, halves, land = (slot[2] * 2 + slot[3]) * BCAP, b_half, b_land
 
-        def one(block, carry):
+        def one(block):
             value = land[(*slot[1:], block)]
             high = value.astype(jnp.bfloat16)
             low = (value - high.astype(jnp.float32)).astype(jnp.bfloat16)
             halves[slot[1], base + block, :, 0:BS] = high
             halves[slot[1], base + block, :, BS : 2 * BS] = low
+
+        def two(step, carry):
+            one(blocks[0] + 2 * step)
+            one(blocks[0] + 2 * step + 1)
             return carry
 
-        lax.fori_loop(*blocks, one, 0)
+        pairs, odd = divmod(blocks[1] - blocks[0], 2)
+        lax.fori_loop(0, pairs, two, 0)
+        if odd:
+            one(blocks[1] - 1)
 
     def multiply(d, total):
         m = lax.rem(o + d, N_LAYER)
@@ -304,21 +311,22 @@
     def collect(d):
         m = lax.rem(o + d, N_LAYER)
 
-        def one(t, carry):
-            at = table_s[16 + m, t]
-            total = jnp.where(
-                jnp.broadcast_to(at, (BS, BS)) < PHASE, chain[jnp.minimum(at, PHASE - 1)], sums[t]
-            )
-            if d == ORDER[-1]:
-                out_ref[t] = total
-            else:
-                sums[t] = total
+        def some(step, carry):
+            for k in range(4):
+                t = step * 4 + k
+                total = chain[table_s[16 + m, t]]
+                if d == ORDER[-1]:
+                    out_ref[t] = total
+                else:
+                    sums[t] = total
+                    chain[PHASE + t] = total
             return carry
 
-        lax.fori_loop(0, CL, one, 0)
+        lax.fori_loop(0, CL // 4, some, 0)
 
     def clear(t, carry):
         sums[t] = jnp.zeros((BS, BS), jnp.float32)
+        chain[PHASE + t] = jnp.zeros((BS, BS), jnp.float32)
         return carry
 
     scalars, running = "none", jnp.zeros((BS, BS), jnp.float32)
@@ -364,7 +372,7 @@
             pltpu.VMEM((N_LAYER, N_X, 2, BCAP, BS, BS), jnp.float32),
             pltpu.VMEM((N_LAYER, N_COL * ACAP, BS, 2 * BS), jnp.bfloat16),
             pltpu.VMEM((N_LAYER, N_ROW * BCAP, BS, 2 * BS), jnp.bfloat16),
-            pltpu.VMEM((PHASE + BCAP, BS, BS), jnp.float32),
+            pltpu.VMEM((PHASE + CL, BS, BS), jnp.float32),
             pltpu.VMEM((CL, BS, BS), jnp.float32),
             pltpu.VMEM((N_ROW, 3, N_LAYER, PCAP), jnp.int32),
             pltpu.VMEM((N_LAYER, N_ROW), jnp.int32),

time: 59 us -> 58.5 us (level)
  no operation moved by 1% of the time
where the time goes in v4:
time: 58.5 us; the launch traced here: 58.4 us
  Pallas kernels  57.1 us (98%)
  local copies, waits for them, and re-layouts  1.32 us (2%)
    pallas_call x1, Pallas kernels, per_device(): pl.pallas_call(kernel, out_shape=jax.ShapeDtypeStruct((CL, BS, BS), jnp.f...  57.1 us
    unnamed x1, local copies, waits for them, and re-layouts  1.32 us

profile of v4, /device:TPU:0, one launch (start us, length us, event | category | flops | bytes accessed | tf_op | source)
XLA Modules:
  0.0 58.4 jit_solution(17393145360671705604)
XLA Ops:
  0.0 57.1 %gather_multiply.1 = f32[32,128,128]{2,1,0:T(8,128)S(1)} custom-call(f32[8,128,128]{2,1,0:T(8,128)} %bitcast.10, f32[4,128,128]{2,1,0:T(8,128)} %bitcast.11, s32[8,3,4,16]{3,2,1,0:T(4,128)} %bitcast.12, s32[4,8]{1,0:T(4,128)} %bitcast.13), custom_call_target="tpu_custom_call" | custom-call | tf_op jit(solution)/shard_map/gather_multiply/pallas_call | solution.py:365
  57.1 1.3 %copy.6 = f32[1,1,32,128,128]{4,3,2,1,0:T(8,128)} copy(f32[1,1,32,128,128]{4,3,2,1,0:T(8,128)S(1)} %bitcast.9) | data formatting | bytes 4194304

commit v5 on v4

--- a/solution.py
+++ b/solution.py
@@ -57,14 +57,18 @@
     fifth = {3: ["Iz3+"], 1: ["Fz3-"], 2: ["Fz3-2"]}
     fourth = {3: ["Fz1+"], 1: ["Iz1-"], 2: ["Fz1+2"]}
     for e in (3, 1, 2):
-        put(f"Gy{e}+2", "Y+", ("A", 3, e), ("A", 2, e), (5, 8), [f"Gy{e}+"] + fifth[e])
+        stop = 7 if e == 2 else 8
+        put(f"Gy{e}+2", "Y+", ("A", 3, e), ("A", 2, e), (5, stop), [f"Gy{e}+"] + fifth[e])
         put(f"Gy{e}-2", "Y-", ("A", 1, e), ("A", 2, e), (4, 5), fourth[e])
     put("Fz2+", "Z+", ("A", 2, 0), ("A", 2, 3), (0, 2), ["Fy+2"])
     put("Fz2-", "Z-", ("A", 2, 0), ("A", 2, 1), (2, 4), ["Fy+2"])
     put("Iz2+", "Z+", ("A", 2, 0), ("A", 2, 3), (2, 4), ["Fy+2"])
     put("Iz2-", "Z-", ("A", 2, 0), ("A", 2, 1), (0, 2), ["Fy+2"])
-    put("Fz2+2", "Z+", ("A", 2, 3), ("A", 2, 2), (0, 2), ["Fz2+"])
-    put("Fz2-2", "Z-", ("A", 2, 1), ("A", 2, 2), (2, 4), ["Fz2-"])
+    put("Jy2+2", "Y+", ("A", 3, 2), ("A", 2, 2), (7, 8), ["Gy2+"])
+    put("Fz2+2", "Z+", ("A", 2, 3), ("A", 2, 2), (0, 1), ["Fz2+"])
+    put("Fz2-2", "Z-", ("A", 2, 1), ("A", 2, 2), (2, 3), ["Fz2-"])
+    put("Jz2+2", "Z+", ("A", 2, 3), ("A", 2, 2), (1, 2), ["Fz2+"])
+    put("Jz2-2", "Z-", ("A", 2, 1), ("A", 2, 2), (3, 4), ["Fz2-"])
     put("By+", "Y+", ("B", 0, 0, 0), ("B", 3, 0, 0), (0, 4), [])
     put("By-", "Y-", ("B", 0, 0, 0), ("B", 1, 0, 0), (0, 4), [])
     put("By+2", "Y+", ("B", 3, 0, 0), ("B", 2, 0, 0), (0, 2), ["By+"])
@@ -82,10 +86,10 @@
 
 
 Z_ORDER = (
-    "Gz*", "Iz*", "Gz*2", "Fz3*", "Iz3*", "Fz3*2", "Fz1*", "Iz1*", "Fz1*2", "Fz2*", "Iz2*", "Fz2*2",
+    "Gz*", "Iz*", "Gz*2", "Fz3*", "Iz3*", "Fz3*2", "Fz1*", "Iz1*", "Fz1*2", "Fz2*", "Iz2*", "Fz2*2", "Jz2*2",
 )
 Y_ORDER = (
-    "By*", "Fy*", "Hy*", "By*2", "Gy3*", "Gy1*", "Gy2*", "Fy*2", "Gy3*2", "Gy1*2", "Gy2*2",
+    "By*", "Fy*", "Hy*", "By*2", "Gy3*", "Gy1*", "Gy2*", "Fy*2", "Gy3*2", "Gy1*2", "Gy2*2", "Jy2*2",
 )
 X_ORDER = ("Bx0*", "Bx0*2", "Bx3*", "Bx1*", "Bx3*2", "Bx1*2", "Bx2*", "Bx2*2")
 
@@ -117,7 +121,7 @@
         steps.append(("send", name))
 
     order = {
-        axis + sign: [n.replace("*", sign) for n in names]
+        axis + sign: [n.replace("*", sign) for n in names if n.replace("*", sign) in table]
         for axis, names in (("Z", Z_ORDER), ("Y", Y_ORDER), ("X", X_ORDER))
         for sign in "+-"
     }

time: 58.5 us -> 58.5 us (level)
  no operation moved by 1% of the time
where the time goes in v5:
time: 58.5 us; the launch traced here: 58.4 us
  Pallas kernels  57.1 us (98%)
  local copies, waits for them, and re-layouts  1.32 us (2%)
    pallas_call x1, Pallas kernels, per_device(): pl.pallas_call(kernel, out_shape=jax.ShapeDtypeStruct((CL, BS, BS), jnp.f...  57.1 us
    unnamed x1, local copies, waits for them, and re-layouts  1.32 us

profile of v5, /device:TPU:0, one launch (start us, length us, event | category | flops | bytes accessed | tf_op | source)
XLA Modules:
  0.0 58.4 jit_solution(1720385660271907728)
XLA Ops:
  0.0 57.1 %gather_multiply.1 = f32[32,128,128]{2,1,0:T(8,128)S(1)} custom-call(f32[8,128,128]{2,1,0:T(8,128)} %bitcast.10, f32[4,128,128]{2,1,0:T(8,128)} %bitcast.11, s32[8,3,4,16]{3,2,1,0:T(4,128)} %bitcast.12, s32[4,8]{1,0:T(4,128)} %bitcast.13), custom_call_target="tpu_custom_call" | custom-call | tf_op jit(solution)/shard_map/gather_multiply/pallas_call | solution.py:369
  57.1 1.3 %copy.6 = f32[1,1,32,128,128]{4,3,2,1,0:T(8,128)} copy(f32[1,1,32,128,128]{4,3,2,1,0:T(8,128)S(1)} %bitcast.9) | data formatting | bytes 4194304
